TPU v7x, 32 devices: a whole 2x2x4 slice. The times are simulated.
32 devices in a mesh: grp: 4 (over y, x), dev: 8 (over z, core).
Axes of the slice: x: 2, y: 2, z: 4, core: 2. Of those that a mesh axis runs over, the one named last changes fastest.
Arguments:
- nz_user: int32 [4096, 128], P(('grp', 'dev')), may hold values from 0 to 8191
- nz_sub: int32 [4096, 128], P(('grp', 'dev')), may hold values from 0 to 2047
- nz_value: float32 [4096, 128], P(('grp', 'dev')), may hold values from -1 to 1
- tile_word: int32 [4096], P(('grp', 'dev')), may hold values from 0 to 2047, as said below
- word_owner: int32 [2048], replicated, may hold values from 0 to 2047, as said below
- user_factor: bfloat16 [64, 8192], P(None, 'dev'), may hold values from -6 to 6
- sub_factor: bfloat16 [64, 2048], P(None, 'dev'), may hold values from -6 to 6
Outputs:
- word_rows: float32 [64, 2048], P(None, ('grp', 'dev'))
Inputs may be any that keep to these rules, and one draw needn't show every extreme that they name: A permutation of the word indices: word w is summed into column word_owner[w] of word_rows. `tile_word`: tile i lies on device i // 128 (grp+dev order). On every device at most 2 tiles belong to words whose output column lies on any one other device, and on every device that bound is reached for some other device.
All inputs are finite; a program needn't handle non-finite values.
Results may differ from a plain program's by a relative error of at most 0.0003.
Values may be sent and summed in bfloat16 or wider, within the bound.
A program may use at most 64 MiB of HBM per device.

v0:
```python
import jax
import jax.numpy as jnp
from jax import lax
from jax.sharding import PartitionSpec as P

CAP = 2


def tile_sums(user_table, sub_table, nz_user, nz_sub, nz_value):
    tile_count, tile_width = nz_user.shape
    block_tiles = min(tile_count, 128)
    block_count = tile_count // block_tiles

    def one_block(block_args):
        users_block, subs_block, vals_block = block_args
        user_rows = jnp.take(user_table, users_block, axis=0).astype(jnp.float32)
        sub_rows = jnp.take(sub_table, subs_block, axis=0).astype(jnp.float32)
        return jnp.sum(user_rows * sub_rows * vals_block[:, :, None], axis=1)

    block_sums = lax.map(
        one_block,
        (
            nz_user.reshape(block_count, block_tiles, tile_width),
            nz_sub.reshape(block_count, block_tiles, tile_width),
            nz_value.reshape(block_count, block_tiles, tile_width),
        ),
    )
    return block_sums.reshape(tile_count, block_sums.shape[2])


def shards(nz_user, nz_sub, nz_value, tile_word, word_owner, user_factor, sub_factor):
    users_all, subs_all = (
        lax.all_gather(user_factor, "dev", axis=1, tiled=True),
        lax.all_gather(sub_factor, "dev", axis=1, tiled=True),
    )
    user_table = jnp.transpose(users_all)
    sub_table = jnp.transpose(subs_all)
    tile_rows = tile_sums(user_table, sub_table, nz_user, nz_sub, nz_value)
    tile_count, rank_width = tile_rows.shape
    grp_size = lax.axis_size("grp")
    dev_size = lax.axis_size("dev")
    devices_all = grp_size * dev_size
    words_total = word_owner.shape[0]
    words_local = words_total // devices_all
    out_rows = jnp.take(word_owner, tile_word)
    self_index = lax.axis_index("grp") * dev_size + lax.axis_index("dev")
    owner_dev = out_rows // words_local
    local_row = out_rows - owner_dev * words_local
    owned = owner_dev == self_index
    columns = jnp.arange(words_local, dtype=jnp.int32)
    own_table = (owned[:, None] & (local_row[:, None] == columns[None, :])).astype(jnp.float32)
    own_part = jnp.einsum("tr,tk->rk", tile_rows, own_table, precision=lax.Precision.HIGHEST)
    peer_ids = jnp.arange(devices_all, dtype=jnp.int32)
    outgoing = (jnp.logical_not(owned)[:, None] & (owner_dev[:, None] == peer_ids[None, :])).astype(
        jnp.float32
    )
    tile_ids = jnp.arange(tile_count, dtype=jnp.int32)
    earlier_table = (tile_ids[:, None] > tile_ids[None, :]).astype(jnp.float32)
    earlier = jnp.dot(
        earlier_table, outgoing, precision=lax.Precision.HIGHEST, preferred_element_type=jnp.float32
    )
    position = jnp.sum(earlier * outgoing, axis=1).astype(jnp.int32)
    send_slot = jnp.where(owned, devices_all * CAP, owner_dev * CAP + position)
    slot_ids = jnp.arange(devices_all * CAP, dtype=jnp.int32)
    slot_table = (send_slot[:, None] == slot_ids[None, :]).astype(jnp.float32)
    send_rows = jnp.einsum("ts,tr->sr", slot_table, tile_rows, precision=lax.Precision.HIGHEST)
    filled = jnp.sum(slot_table, axis=0)
    send_ids = (
        jnp.dot(
            local_row.astype(jnp.float32),
            slot_table,
            precision=lax.Precision.HIGHEST,
            preferred_element_type=jnp.float32,
        )
        + filled
        - 1.0
    )
    send_rows = send_rows.reshape(grp_size, dev_size, CAP * rank_width)
    send_ids = send_ids.reshape(grp_size, dev_size, CAP)
    got_rows, got_ids = (
        lax.all_to_all(
            lax.all_to_all(send_rows, "grp", split_axis=0, concat_axis=0, tiled=True),
            "dev",
            split_axis=1,
            concat_axis=1,
            tiled=True,
        ),
        lax.all_to_all(
            lax.all_to_all(send_ids, "grp", split_axis=0, concat_axis=0, tiled=True),
            "dev",
            split_axis=1,
            concat_axis=1,
            tiled=True,
        ),
    )
    got_rows = got_rows.reshape(devices_all * CAP, rank_width)
    got_ids = got_ids.reshape(devices_all * CAP).astype(jnp.int32)
    got_table = (got_ids[:, None] == columns[None, :]).astype(jnp.float32)
    far_part = jnp.einsum("sr,sk->rk", got_rows, got_table, precision=lax.Precision.HIGHEST)
    return own_part + far_part


def solution(mesh):
    return jax.shard_map(
        shards,
        mesh=mesh,
        in_specs=(
            P(("grp", "dev"), None),
            P(("grp", "dev"), None),
            P(("grp", "dev"), None),
            P(("grp", "dev")),
            P(),
            P(None, "dev"),
            P(None, "dev"),
        ),
        out_specs=P(None, ("grp", "dev")),
        check_vma=False,
    )
```

profile of v0, /device:TPU:0, one launch (start us, length us, event | category | flops | bytes accessed | tf_op | source)
XLA Modules:
  0.0 198.2 jit_solution(13226460569784429638)
XLA Ops:
  6.5 1.8 copy.39
  8.3 0.7 compare_select_fusion.2
  9.0 1.1 gather_fusion.2
  10.2 0.7 fusion.16
  10.8 0.2 fusion
  11.0 0.7 add_select_fusion
  11.7 0.1 convert_reduce_fusion
  11.8 0.1 fusion.2
  11.9 0.1 reshape.81
  12.1 0.7 copy.43
  12.7 5.2 %all-to-all-start.2 = ((f32[4,8,2]{1,2,0:T(2,128)}), f32[4,8,2]{1,2,0:T(2,128)S(1)}, u32[]{:S(2)}, u32[]{:S(2)}) async-start(f32[4,8,2]{1,2,0:T(2,128)} %copy.43), calls=%async_computation.2 | async-start | bytes 8192 | tf_op jit(solution)/shard_map/all_to_all | solution.py:89
  17.9 0.9 copy.40
  18.8 0.9 compare_and_fusion
  19.7 0.9 bitcast_clamp_fusion.1
  20.6 0.9 bitcast_clamp_fusion
  21.5 17.7 %all_gather.7 = bf16[64,2048]{0,1:T(8,128)(2,1)S(1)} all-gather(bf16[64,256]{0,1:T(8,128)(2,1)S(1)} %copy.40), channel_id=1, replica_groups=mesh['grp'=4,'dev'=8] {'dev'}, dimensions={1}, use_global_device_ids=true | all-gather | bytes 294912 | tf_op jit(solution)/shard_map/all_gather | solution.py:34
  39.1 57.4 %gather_fusion.1 = bf16[16384,64]{1,0:T(8,128)(2,1)} fusion(bf16[2048,64]{1,0:T(8,128)(2,1)S(1)} %bitcast.22, s32[16384]{0:T(1024)S(1)} %bitcast_clamp_fusion), kind=kCustom, calls=%fused_computation.1 | custom fusion | bytes 4259840 | tf_op jit(solution)/shard_map/while/body/eval_jaxpr/jit(_take)/gather | solution.py:17
  96.5 0.7 copy.44
  97.2 4.8 %all-to-all-start.3 = ((f32[4,8,2]{0,2,1:T(2,128)}), f32[4,8,2]{0,2,1:T(2,128)S(1)}, u32[]{:S(2)}, u32[]{:S(2)}) async-start(f32[4,8,2]{0,2,1:T(2,128)} %copy.44), calls=%async_computation.3 | async-start | bytes 16384 | tf_op jit(solution)/shard_map/all_to_all | solution.py:88
  102.0 56.8 %gather_fusion = bf16[16384,64]{1,0:T(8,128)(2,1)} fusion(bf16[8192,64]{1,0:T(8,128)(2,1)} %bitcast.23, s32[16384]{0:T(1024)S(1)} %bitcast_clamp_fusion.1), kind=kCustom, calls=%fused_computation | custom fusion | bytes 4259840 | tf_op jit(solution)/shard_map/while/body/eval_jaxpr/jit(_take)/gather | solution.py:16
  158.8 10.6 %multiply_reduce_fusion = f32[128,64]{1,0:T(8,128)S(1)} fusion(f32[128,128]{1,0:T(8,128)S(1)} %copy-done.1, pred[128,128]{1,0:T(8,128)(4,1)S(1)} %get-tuple-element.30, pred[128,128]{1,0:T(8,128)(4,1)S(1)} %get-tuple-element.32, bf16[16384,64]{1,0:T(8,128)(2,1)} %gather_fusion.1, bf16[16384,64]{1,0:T(8,128)(2,1)} %gather_fusion), kind=kLoop, calls=%fused_computation.3 | loop fusion | flops 7331840 | bytes 4325376 | tf_op jit(solution)/shard_map/while/body/eval_jaxpr/reduce_sum | solution.py:18
  169.4 0.2 fusion.6
  169.6 0.7 reshape.79
  170.3 4.1 %all-to-all-start = ((f32[4,8,128]{2,1,0:T(8,128)}), f32[4,8,128]{2,1,0:T(8,128)S(1)}, u32[]{:S(2)}, u32[]{:S(2)}) async-start(f32[4,8,128]{2,1,0:T(8,128)} %reshape.79), calls=%async_computation | async-start | bytes 32768 | tf_op jit(solution)/shard_map/all_to_all | solution.py:82
  174.5 0.1 copy.46
  174.6 0.1 convert_element_type.39
  174.7 4.4 %all-to-all-done = f32[4,8,128]{2,1,0:T(8,128)S(1)} async-done(((f32[4,8,128]{2,1,0:T(8,128)}), f32[4,8,128]{2,1,0:T(8,128)S(1)}, u32[]{:S(2)}, u32[]{:S(2)}) %all-to-all-start) | async-done | bytes 16416 | tf_op jit(solution)/shard_map/all_to_all | solution.py:82
  179.1 0.6 copy.41
  179.7 5.1 %all-to-all-start.1 = ((f32[4,8,128]{2,0,1:T(4,128)}), f32[4,8,128]{2,0,1:T(4,128)S(1)}, u32[]{:S(2)}, u32[]{:S(2)}) async-start(f32[4,8,128]{2,0,1:T(4,128)} %copy.41), calls=%async_computation.1 | async-start | bytes 32768 | tf_op jit(solution)/shard_map/all_to_all | solution.py:81
  184.8 0.3 fusion.4
  185.1 5.4 %all-to-all-done.1 = f32[4,8,128]{2,0,1:T(4,128)S(1)} async-done(((f32[4,8,128]{2,0,1:T(4,128)}), f32[4,8,128]{2,0,1:T(4,128)S(1)}, u32[]{:S(2)}, u32[]{:S(2)}) %all-to-all-start.1) | async-done | bytes 16416 | tf_op jit(solution)/shard_map/all_to_all | solution.py:81
  190.5 0.9 convolution_add_fusion
  (14 shorter events, 0.2 us)
Async XLA Ops:
  6.5 2.5 %copy-start = (s32[2048]{0:T(1024)S(1)}, s32[2048]{0:T(1024)}, u32[]{:S(2)}) copy-start(s32[2048]{0:T(1024)} %param.11) | copy-start | bytes 24580
  6.5 95.5 %all-gather.2.cloned.1.call-start = ((), (), s32[]{:S(2)}) async-start(), calls=%async_computation.4 | async-start | bytes 2359296 | tf_op jit(solution)/shard_map/all_gather | solution.py:33
  12.7 83.8 %all-to-all-start.2 = ((f32[4,8,2]{1,2,0:T(2,128)}), f32[4,8,2]{1,2,0:T(2,128)S(1)}, u32[]{:S(2)}, u32[]{:S(2)}) async-start(f32[4,8,2]{1,2,0:T(2,128)} %copy.43), calls=%async_computation.2 | async-start | bytes 8192 | tf_op jit(solution)/shard_map/all_to_all | solution.py:89
  97.2 73.1 %all-to-all-start.3 = ((f32[4,8,2]{0,2,1:T(2,128)}), f32[4,8,2]{0,2,1:T(2,128)S(1)}, u32[]{:S(2)}, u32[]{:S(2)}) async-start(f32[4,8,2]{0,2,1:T(2,128)} %copy.44), calls=%async_computation.3 | async-start | bytes 16384 | tf_op jit(solution)/shard_map/all_to_all | solution.py:88
  102.0 56.8 %copy-start.1 = (f32[128,128]{1,0:T(8,128)S(1)}, f32[128,128]{1,0:T(8,128)}, u32[]{:S(2)}) copy-start(f32[128,128]{1,0:T(8,128)} %param.9) | copy-start | bytes 196612
  170.3 8.8 %all-to-all-start = ((f32[4,8,128]{2,1,0:T(8,128)}), f32[4,8,128]{2,1,0:T(8,128)S(1)}, u32[]{:S(2)}, u32[]{:S(2)}) async-start(f32[4,8,128]{2,1,0:T(8,128)} %reshape.79), calls=%async_computation | async-start | bytes 32768 | tf_op jit(solution)/shard_map/all_to_all | solution.py:82
  179.7 10.7 %all-to-all-start.1 = ((f32[4,8,128]{2,0,1:T(4,128)}), f32[4,8,128]{2,0,1:T(4,128)S(1)}, u32[]{:S(2)}, u32[]{:S(2)}) async-start(f32[4,8,128]{2,0,1:T(4,128)} %copy.41), calls=%async_computation.1 | async-start | bytes 32768 | tf_op jit(solution)/shard_map/all_to_all | solution.py:81
Sparse Core Ops, SparseCore 0:
  8.9 36.0 all-gather.1
where the time goes:
time: 199 us; the launch traced here: 198 us
  local copies, waits for them, and re-layouts  121 us (61%)
  starting transfers between devices  19.2 us (10%)
  blocking collectives  17.7 us (9%)
  other arithmetic  15.4 us (8%)
  between operations  13.5 us (7%)
  waiting for transfers between devices  9.81 us (5%)
    gather x1, local copies, waits for them, and re-layouts, one_block(): sub_rows = jnp.take(sub_table, subs_block, axis=0).astype(jnp.float32)  57.4 us
    gather x1, local copies, waits for them, and re-layouts, one_block(): user_rows = jnp.take(user_table, users_block, axis=0).astype(jnp.float32)  56.8 us
    all_gather x1, blocking collectives, shards(): lax.all_gather(sub_factor, 'dev', axis=1, tiled=True)  17.7 us
    reduce_sum x1, other arithmetic, one_block(): return jnp.sum(user_rows * sub_rows * vals_block[:, :, None], axis=1)  10.6 us
    all_to_all x1, waiting for transfers between devices, shards(): lax.all_to_all(lax.all_to_all(send_rows, 'grp', split_axis=0, concat_axis...  5.38 us
    all_to_all x1, starting transfers between devices, shards(): lax.all_to_all(send_ids, 'grp', split_axis=0, concat_axis=0, tiled=True)  5.19 us
    all_to_all x1, starting transfers between devices, shards(): lax.all_to_all(lax.all_to_all(send_rows, 'grp', split_axis=0, concat_axis...  5.08 us
    all_to_all x1, starting transfers between devices, shards(): lax.all_to_all(lax.all_to_all(send_ids, 'grp', split_axis=0, concat_axis=...  4.77 us
  transfers between devices with their start and end apart: 5, of which 2 were waited for; matrix products, arithmetic and copies ran while one was open for 68% of the time, Pallas kernels for 0%

commit v1 on v0

v1 whole, which is shorter than its diff:
```python
import functools
import jax
import jax.numpy as jnp
from jax import lax
from jax.experimental import pallas as pl
from jax.experimental.pallas import tpu as pltpu

CAP = 2
LANES = 128
VMEM = pltpu.VMEM
HIGH = lax.Precision.HIGHEST
MESH = pl.DeviceIdType.MESH


def packed(x):
    half = x.shape[1] // 2
    x = x.astype(jnp.float32)
    return jnp.concatenate([x[:, :half], x[:, half:]], axis=0).T.astype(jnp.bfloat16)


def gather_kernel(n_grp, n_dev, uf_ref, sf_ref, out_ref, send_a, recv_a, send_b, recv_b, send_c, recv_c):
    grp, dev = lax.axis_index("grp"), lax.axis_index("dev")
    pairs = n_dev // 2
    pos, core = dev // 2, lax.rem(dev, 2)
    sibling = dev + 1 - 2 * core
    rows = out_ref.shape[2]
    barrier = pltpu.get_barrier_semaphore()
    order = sorted(range(1, pairs), key=lambda k: min(k, pairs - k))
    others = [((pos + k) % pairs) for k in order]
    groups = [lax.rem(grp + j, n_grp) for j in range(1, n_grp)]
    for p in others:
        pl.semaphore_signal(barrier, inc=1, device_id=(grp, 2 * p + core), device_id_type=MESH)
    for g in groups:
        pl.semaphore_signal(barrier, inc=1, device_id=(g, dev), device_id_type=MESH)
    pl.semaphore_signal(barrier, inc=1, device_id=(grp, sibling), device_id_type=MESH)

    block = jnp.concatenate([packed(uf_ref[...]), packed(sf_ref[...])], axis=0)
    for q in range(n_grp):
        out_ref[q, dev] = block[q * rows:(q + 1) * rows]
    pl.semaphore_wait(barrier, len(others) + len(groups) + 1)

    def copy(q, d, send, recv, to):
        return pltpu.make_async_remote_copy(
            src_ref=out_ref.at[q, d], dst_ref=out_ref.at[q, d], send_sem=send, recv_sem=recv,
            device_id=to, device_id_type=MESH)

    sent = []

    def start(c):
        c.start()
        sent.append(c)

    def to_sibling(q, p):
        start(copy(q, 2 * p + core, send_c.at[q, p], recv_c.at[q, p], (grp, sibling)))

    for p in others:
        start(copy(grp, dev, send_a.at[p], recv_a.at[pos], (grp, 2 * p + core)))
    for q in range(n_grp):
        to_sibling(q, pos)
    for p in others:
        d = 2 * p + core
        copy(grp, d, send_a.at[p], recv_a.at[p], (grp, d)).wait_recv()
        for g in groups:
            start(copy(grp, d, send_b.at[g, p], recv_b.at[grp, p], (g, dev)))
        to_sibling(grp, p)
    for p in others:
        for g in groups:
            d = 2 * p + core
            copy(g, d, send_b.at[g, p], recv_b.at[g, p], (g, dev)).wait_recv()
            to_sibling(g, p)
    for p in [pos] + others:
        for q in range(n_grp):
            copy(q, 2 * p + (1 - core), send_c.at[q, p], recv_c.at[q, p], (grp, sibling)).wait_recv()
    for c in sent:
        c.wait_send()


def gather_tables(n_grp, n_dev, uf, sf):
    rows = (uf.shape[1] + sf.shape[1]) // 2 // n_grp
    pairs = n_dev // 2
    dma = pltpu.SemaphoreType.DMA
    return pl.pallas_call(
        functools.partial(gather_kernel, n_grp, n_dev),
        out_shape=jax.ShapeDtypeStruct((n_grp, n_dev, rows, LANES), jnp.bfloat16),
        in_specs=[pl.BlockSpec(memory_space=VMEM)] * 2,
        out_specs=pl.BlockSpec(memory_space=VMEM),
        scratch_shapes=[dma((pairs,)), dma((pairs,)), dma((n_grp, pairs)), dma((n_grp, pairs)),
                        dma((n_grp, pairs)), dma((n_grp, pairs))],
        compiler_params=pltpu.CompilerParams(collective_id=0, has_side_effects=True),
        name="gather_tables",
    )(uf, sf)


def tile_kernel(user_dev, sub_dev, tab_ref, val_ref, user_hbm, sub_hbm, word_hbm, owner_hbm, out_ref,
                utab, stab, vt, prod, users, subs, words, owners, sems):
    copies = [pltpu.make_async_copy(src, dst, sems.at[i]) for i, (src, dst) in enumerate(
        [(user_hbm, users), (sub_hbm, subs), (word_hbm, words), (owner_hbm, owners)])]
    for c in copies:
        c.start()
    n_grp, n_dev, rows, lanes = tab_ref.shape
    tiles, width = users.shape
    rank = lanes // 2
    user_half, sub_half = user_dev // 2, sub_dev // 2

    def fill(d, carry):
        for q in range(n_grp):
            lo, hi = q * rows, (q + 1) * rows
            for table, first, last, size in ((utab, 0, user_half, user_dev),
                                             (stab, user_half, user_half + sub_half, sub_dev)):
                a, b = max(lo, first), min(hi, last)
                if a >= b:
                    continue
                x = tab_ref[q, d, a - lo:b - lo, :].astype(jnp.float32)
                base = d * size + (a - first)
                table[pl.ds(pl.multiple_of(base, 8), b - a), :] = x
                table[pl.ds(pl.multiple_of(base + size // 2, 8), b - a), :] = pltpu.roll(x, rank, 1)
        return carry

    lax.fori_loop(0, n_dev, fill, 0)
    vt[...] = val_ref[...].T
    for c in copies:
        c.wait()
    lane = lax.broadcasted_iota(jnp.int32, (1, lanes), 1)

    def one_tile(t, carry):
        for n in range(width):
            u, s = users[t, n], subs[t, n]
            prod[n:n + 1, :] = utab[pl.ds(u, 1), :] * stab[pl.ds(s, 1), :]
        vals = pltpu.roll(vt[...], tiles - t, 1)[:, 0:1]
        row = jnp.sum(prod[...] * vals, axis=0, keepdims=True)
        owner = owners[words[t]].astype(jnp.float32)
        out_ref[pl.ds(t, 1), :] = jnp.where(lane < rank, row, owner)
        return carry

    lax.fori_loop(0, tiles, one_tile, 0)


def tile_rows(tables, user_dev, sub_dev, nz_user, nz_sub, nz_value, tile_word, word_owner):
    tiles, width = nz_user.shape
    n_dev = tables.shape[1]
    any_spec = pl.BlockSpec(memory_space=pl.ANY)
    vmem = pl.BlockSpec(memory_space=VMEM)
    return pl.pallas_call(
        functools.partial(tile_kernel, user_dev, sub_dev),
        out_shape=jax.ShapeDtypeStruct((tiles, LANES), jnp.float32),
        in_specs=[vmem, vmem, any_spec, any_spec, any_spec, any_spec],
        out_specs=vmem,
        scratch_shapes=[
            VMEM((user_dev * n_dev, LANES), jnp.float32),
            VMEM((sub_dev * n_dev, LANES), jnp.float32),
            VMEM((width, tiles), jnp.float32),
            VMEM((width, LANES), jnp.float32),
            pltpu.SMEM(nz_user.shape, jnp.int32),
            pltpu.SMEM(nz_sub.shape, jnp.int32),
            pltpu.SMEM(tile_word.shape, jnp.int32),
            pltpu.SMEM(word_owner.shape, jnp.int32),
            pltpu.SemaphoreType.DMA((4,)),
        ],
        compiler_params=pltpu.CompilerParams(vmem_limit_bytes=63_000_000),
        name="tile_rows",
    )(tables, nz_value, nz_user, nz_sub, tile_word, word_owner)


def tdot(a, b):
    return lax.dot_general(a, b, (((0,), (0,)), ((), ())), precision=HIGH,
                           preferred_element_type=jnp.float32)


def exchange_kernel(n_grp, n_dev, cols, rows_ref, out_ref, outbox, inbox, send_sem, recv_sem):
    grp, dev = lax.axis_index("grp"), lax.axis_index("dev")
    n_all = n_grp * n_dev
    me = grp * n_dev + dev
    barrier = pltpu.get_barrier_semaphore()
    peers = [lax.rem(me + k, n_all) for k in range(1, n_all)]

    def where_is(p):
        return (p // n_dev, lax.rem(p, n_dev))

    for p in peers:
        pl.semaphore_signal(barrier, inc=1, device_id=where_is(p), device_id_type=MESH)
    rows = rows_ref[...]
    tiles, lanes = rows.shape
    rank = lanes // 2
    lane = lax.broadcasted_iota(jnp.int32, (tiles, lanes), 1)
    owner_row = jnp.where(lane < rank, pltpu.roll(rows, rank, 1), rows).astype(jnp.int32)
    owner = owner_row // cols
    local = owner_row - owner * cols
    slots = n_all * CAP
    slot = lax.broadcasted_iota(jnp.int32, (tiles, slots), 1)
    own_col = owner_row[:, :1]
    owner_col = jnp.broadcast_to(owner[:, :1], (tiles, slots))
    going = jnp.where((owner_col != me) & (owner_col == slot // CAP), 1.0, 0.0)
    earlier = jnp.where(lax.broadcasted_iota(jnp.int32, (tiles, tiles), 0)
                        > lax.broadcasted_iota(jnp.int32, (tiles, tiles), 1), 1.0, 0.0)
    before = jnp.dot(earlier.astype(jnp.bfloat16), going.astype(jnp.bfloat16),
                     preferred_element_type=jnp.float32)
    table = jnp.where(before == (slot - slot // CAP * CAP).astype(jnp.float32), going, 0.0)
    tagged = jnp.where(lane < rank, rows, (local + 1).astype(jnp.float32))
    box = tdot(table, tagged)
    for p in range(n_all):
        outbox[p] = box[p * CAP:(p + 1) * CAP]
    inbox[me] = jnp.zeros((CAP, lanes), jnp.float32)
    pl.semaphore_wait(barrier, n_all - 1)
    copies = []
    for p in peers:
        c = pltpu.make_async_remote_copy(
            src_ref=outbox.at[p], dst_ref=inbox.at[me], send_sem=send_sem.at[p],
            recv_sem=recv_sem.at[me], device_id=where_is(p), device_id_type=MESH)
        c.start()
        copies.append(c)
    col = lax.broadcasted_iota(jnp.int32, (tiles, lanes), 1)
    mine = jnp.where(owner_row == me * cols + col, 1.0, 0.0)
    own_part = tdot(rows, mine)
    for p in peers:
        pltpu.make_async_remote_copy(
            src_ref=outbox.at[p], dst_ref=inbox.at[p], send_sem=send_sem.at[p],
            recv_sem=recv_sem.at[p], device_id=where_is(p), device_id_type=MESH).wait_recv()
    got = jnp.concatenate([inbox[p] for p in range(n_all)], axis=0)
    glane = lax.broadcasted_iota(jnp.int32, (slots, lanes), 1)
    got_row = jnp.where(glane < rank, pltpu.roll(got, rank, 1), got).astype(jnp.int32)
    far_part = tdot(got, jnp.where(got_row == glane + 1, 1.0, 0.0))
    out_ref[...] = (own_part + far_part)[:rank, :cols]
    for c in copies:
        c.wait_send()


def exchange(n_grp, n_dev, cols, rows):
    n_all = n_grp * n_dev
    rank = rows.shape[1] // 2
    return pl.pallas_call(
        functools.partial(exchange_kernel, n_grp, n_dev, cols),
        out_shape=jax.ShapeDtypeStruct((rank, cols), jnp.float32),
        in_specs=[pl.BlockSpec(memory_space=VMEM)],
        out_specs=pl.BlockSpec(memory_space=VMEM),
        scratch_shapes=[
            VMEM((n_all, CAP, LANES), jnp.float32),
            VMEM((n_all, CAP, LANES), jnp.float32),
            pltpu.SemaphoreType.DMA((n_all,)),
            pltpu.SemaphoreType.DMA((n_all,)),
        ],
        compiler_params=pltpu.CompilerParams(collective_id=1, has_side_effects=True),
        name="exchange",
    )(rows)


def solution(mesh):
    n_grp, n_dev = mesh.shape["grp"], mesh.shape["dev"]

    def shards(nz_user, nz_sub, nz_value, tile_word, word_owner, user_factor, sub_factor):
        tables = gather_tables(n_grp, n_dev, user_factor, sub_factor)
        rows = tile_rows(tables, user_factor.shape[1], sub_factor.shape[1],
                         nz_user, nz_sub, nz_value, tile_word, word_owner)
        return exchange(n_grp, n_dev, word_owner.shape[0] // (n_grp * n_dev), rows)

    return jax.shard_map(
        shards,
        mesh=mesh,
        in_specs=(
            jax.sharding.PartitionSpec(("grp", "dev"), None),
            jax.sharding.PartitionSpec(("grp", "dev"), None),
            jax.sharding.PartitionSpec(("grp", "dev"), None),
            jax.sharding.PartitionSpec(("grp", "dev")),
            jax.sharding.PartitionSpec(),
            jax.sharding.PartitionSpec(None, "dev"),
            jax.sharding.PartitionSpec(None, "dev"),
        ),
        out_specs=jax.sharding.PartitionSpec(None, ("grp", "dev")),
        check_vma=False,
    )
```

time: 199 us -> 63.3 us (0.32)
  local copies, waits for them, and re-layouts: 121 us -> 1.38 us
  Pallas kernels: 0 us -> 61.5 us
  starting transfers between devices: 19.2 us -> 0 us
  blocking collectives: 17.7 us -> 0 us
  other arithmetic: 15.4 us -> 0 us
  between operations: 13.5 us -> 0.02 us
  waiting for transfers between devices: 9.81 us -> 0 us
    gather x3 -> x0, local copies, waits for them, and re-layouts: 115 us -> none  [the longest x1 57.4 us: one_block(): sub_rows = jnp.take(sub_table, subs_block, axis=0).astype(jnp.float32)]
    pallas_call x0 -> x3, Pallas kernels: none -> 61.5 us  [the longest x1 33.3 us: tile_rows(): pl.pallas_call(functools.partial(tile_kernel, user_dev, sub_dev), out_sha...]
    all_to_all x4 -> x0, starting transfers between devices: 19.2 us -> none  [the longest x1 5.19 us: shards(): lax.all_to_all(send_ids, 'grp', split_axis=0, concat_axis=0, tiled=True)]
    all_gather x1 -> x0, blocking collectives: 17.7 us -> none  [shards(): lax.all_gather(sub_factor, 'dev', axis=1, tiled=True)]
    reduce_sum x2 -> x0, other arithmetic: 10.7 us -> none  [the longest x1 10.6 us: one_block(): return jnp.sum(user_rows * sub_rows * vals_block[:, :, None], axis=1)]
    all_to_all x4 -> x0, waiting for transfers between devices: 9.79 us -> none  [the longest x1 5.38 us: shards(): lax.all_to_all(lax.all_to_all(send_rows, 'grp', split_axis=0, concat_axis...]
  transfers between devices with their start and end apart: 5 -> 0, of which waited for: 2 -> 0; matrix products, arithmetic and copies ran while one was open for 68% -> 0% of each run, Pallas kernels for 0% -> 0%
where the time goes in v1:
time: 63.3 us; the launch traced here: 62.9 us
  Pallas kernels  61.5 us (97%)
  local copies, waits for them, and re-layouts  1.38 us (2%)
    pallas_call x1, Pallas kernels, tile_rows(): pl.pallas_call(functools.partial(tile_kernel, user_dev, sub_dev), out_sha...  33.3 us
    pallas_call x1, Pallas kernels, gather_tables(): pl.pallas_call(functools.partial(gather_kernel, n_grp, n_dev), out_shape=...  18.1 us
    pallas_call x1, Pallas kernels, exchange(): pl.pallas_call(functools.partial(exchange_kernel, n_grp, n_dev, cols), ou...  10.1 us
    unnamed x1, local copies, waits for them, and re-layouts  1.38 us

profile of v1, /device:TPU:0, one launch (start us, length us, event | category | flops | bytes accessed | tf_op | source)
XLA Modules:
  0.0 62.9 jit_solution(2911328112003666145)
XLA Ops:
  0.0 18.1 %gather_tables.1.tab_ref = bf16[4,8,160,128]{3,2,1,0:T(8,128)(2,1)} custom-call(bf16[64,1024]{1,0:T(8,128)(2,1)} %uf_ref.1, bf16[64,256]{1,0:T(8,128)(2,1)} %sf_ref.1), custom_call_target="tpu_custom_call" | custom-call | tf_op jit(solution)/shard_map/gather_tables/pallas_call | solution.py:82
  18.1 33.3 %tile_rows.1.rows_ref = f32[128,128]{1,0:T(8,128)} custom-call(bf16[4,8,160,128]{3,2,1,0:T(8,128)(2,1)} %gather_tables.1.tab_ref, f32[128,128]{1,0:T(8,128)} %val_ref.1, s32[128,128]{1,0:T(8,128)} %user_hbm.1, s32[128,128]{1,0:T(8,128)} %sub_hbm.1, s32[128]{0:T(128)} %word_hbm.1, s32[2048]{0:T(1024)} %owner_hbm.1), custom_call_target="tpu_custom_call" | custom-call | tf_op jit(solution)/shard_map/tile_rows/pallas_call | solution.py:143
  51.4 10.1 %exchange.1 = f32[64,64]{1,0:T(8,128)} custom-call(f32[128,128]{1,0:T(8,128)} %tile_rows.1.rows_ref), custom_call_target="tpu_custom_call" | custom-call | tf_op jit(solution)/shard_map/exchange/pallas_call | solution.py:230
  61.5 1.4 %copy.9 = f32[64,64]{1,0:T(8,128)} copy(f32[64,64]{1,0:T(8,128)} %exchange.1) | data formatting | bytes 32768

commit v2 on v1

--- a/solution.py
+++ b/solution.py
@@ -91,48 +91,87 @@
     )(uf, sf)
 
 
+def fill_tables(tab_ref, d, user_dev, sub_dev, utab, stab):
+    n_grp, _, rows, lanes = tab_ref.shape
+    rank = lanes // 2
+    user_half, sub_half = user_dev // 2, sub_dev // 2
+    for q in range(n_grp):
+        lo, hi = q * rows, (q + 1) * rows
+        for table, first, last, size in ((utab, 0, user_half, user_dev),
+                                         (stab, user_half, user_half + sub_half, sub_dev)):
+            a, b = max(lo, first), min(hi, last)
+            if a >= b:
+                continue
+            x = tab_ref[q, d, a - lo:b - lo, :].astype(jnp.float32)
+            base = d * size + (a - first)
+            table[pl.ds(pl.multiple_of(base, 8), b - a), :] = x
+            table[pl.ds(pl.multiple_of(base + size // 2, 8), b - a), :] = pltpu.roll(x, rank, 1)
+
+
+STEP = 8
+
+
+def index_copies(c, half, user_hbm, sub_hbm, users, subs, sems):
+    rows = pl.ds(pl.multiple_of(c * STEP, STEP), STEP)
+    return [pltpu.make_async_copy(user_hbm.at[rows], users[half], sems.at[half, 0]),
+            pltpu.make_async_copy(sub_hbm.at[rows], subs[half], sems.at[half, 1])]
+
+
+def sum_tiles(user_hbm, sub_hbm, val_ref, words, owners, out_ref, utab, stab, prod, users, subs, sems):
+    tiles, lanes = out_ref.shape
+    rank = lanes // 2
+    width = val_ref.shape[1]
+    chunks = tiles // STEP
+    lane = lax.broadcasted_iota(jnp.int32, (1, lanes), 1)
+
+    def chunk(c, half):
+        for copy in index_copies(c, half, user_hbm, sub_hbm, users, subs, sems):
+            copy.wait()
+        base = pl.multiple_of(c * STEP, STEP)
+        vals = val_ref[pl.ds(base, STEP), :].T
+        out = []
+        for j in range(STEP):
+            for n in range(width):
+                u, s = users[half][j, n], subs[half][j, n]
+                prod[j % 2, n:n + 1, :] = utab[pl.ds(u, 1), :] * stab[pl.ds(s, 1), :]
+            row = jnp.sum(prod[j % 2] * vals[:, j:j + 1], axis=0, keepdims=True)
+            owner = owners[words[base + j]].astype(jnp.float32)
+            out.append(jnp.where(lane < rank, row, owner))
+        out_ref[pl.ds(base, STEP), :] = jnp.concatenate(out, axis=0)
+
+    def two_chunks(i, carry):
+        for half in range(2):
+            c = 2 * i + half
+            chunk(c, half)
+
+            @pl.when(i < chunks // 2 - 1)
+            def _():
+                for copy in index_copies(c + 2, half, user_hbm, sub_hbm, users, subs, sems):
+                    copy.start()
+        return carry
+
+    lax.fori_loop(0, chunks // 2, two_chunks, 0)
+
+
 def tile_kernel(user_dev, sub_dev, tab_ref, val_ref, user_hbm, sub_hbm, word_hbm, owner_hbm, out_ref,
-                utab, stab, vt, prod, users, subs, words, owners, sems):
-    copies = [pltpu.make_async_copy(src, dst, sems.at[i]) for i, (src, dst) in enumerate(
-        [(user_hbm, users), (sub_hbm, subs), (word_hbm, words), (owner_hbm, owners)])]
+                utab, stab, prod, users_a, users_b, subs_a, subs_b, words, owners, sems, word_sems):
+    users, subs = (users_a, users_b), (subs_a, subs_b)
+    copies = [pltpu.make_async_copy(word_hbm, words, word_sems.at[0]),
+              pltpu.make_async_copy(owner_hbm, owners, word_sems.at[1])]
+    for half in range(2):
+        for c in index_copies(half, half, user_hbm, sub_hbm, users, subs, sems):
+            c.start()
     for c in copies:
         c.start()
-    n_grp, n_dev, rows, lanes = tab_ref.shape
-    tiles, width = users.shape
-    rank = lanes // 2
-    user_half, sub_half = user_dev // 2, sub_dev // 2
 
     def fill(d, carry):
-        for q in range(n_grp):
-            lo, hi = q * rows, (q + 1) * rows
-            for table, first, last, size in ((utab, 0, user_half, user_dev),
-                                             (stab, user_half, user_half + sub_half, sub_dev)):
-                a, b = max(lo, first), min(hi, last)
-                if a >= b:
-                    continue
-                x = tab_ref[q, d, a - lo:b - lo, :].astype(jnp.float32)
-                base = d * size + (a - first)
-                table[pl.ds(pl.multiple_of(base, 8), b - a), :] = x
-                table[pl.ds(pl.multiple_of(base + size // 2, 8), b - a), :] = pltpu.roll(x, rank, 1)
+        fill_tables(tab_ref, d, user_dev, sub_dev, utab, stab)
         return carry
 
-    lax.fori_loop(0, n_dev, fill, 0)
-    vt[...] = val_ref[...].T
+    lax.fori_loop(0, tab_ref.shape[1], fill, 0)
     for c in copies:
         c.wait()
-    lane = lax.broadcasted_iota(jnp.int32, (1, lanes), 1)
-
-    def one_tile(t, carry):
-        for n in range(width):
-            u, s = users[t, n], subs[t, n]
-            prod[n:n + 1, :] = utab[pl.ds(u, 1), :] * stab[pl.ds(s, 1), :]
-        vals = pltpu.roll(vt[...], tiles - t, 1)[:, 0:1]
-        row = jnp.sum(prod[...] * vals, axis=0, keepdims=True)
-        owner = owners[words[t]].astype(jnp.float32)
-        out_ref[pl.ds(t, 1), :] = jnp.where(lane < rank, row, owner)
-        return carry
-
-    lax.fori_loop(0, tiles, one_tile, 0)
+    sum_tiles(user_hbm, sub_hbm, val_ref, words, owners, out_ref, utab, stab, prod, users, subs, sems)
 
 
 def tile_rows(tables, user_dev, sub_dev, nz_user, nz_sub, nz_value, tile_word, word_owner):
@@ -148,13 +187,15 @@
         scratch_shapes=[
             VMEM((user_dev * n_dev, LANES), jnp.float32),
             VMEM((sub_dev * n_dev, LANES), jnp.float32),
-            VMEM((width, tiles), jnp.float32),
-            VMEM((width, LANES), jnp.float32),
-            pltpu.SMEM(nz_user.shape, jnp.int32),
-            pltpu.SMEM(nz_sub.shape, jnp.int32),
+            VMEM((2, width, LANES), jnp.float32),
+            pltpu.SMEM((STEP, width), jnp.int32),
+            pltpu.SMEM((STEP, width), jnp.int32),
+            pltpu.SMEM((STEP, width), jnp.int32),
+            pltpu.SMEM((STEP, width), jnp.int32),
             pltpu.SMEM(tile_word.shape, jnp.int32),
             pltpu.SMEM(word_owner.shape, jnp.int32),
-            pltpu.SemaphoreType.DMA((4,)),
+            pltpu.SemaphoreType.DMA((2, 2)),
+            pltpu.SemaphoreType.DMA((2,)),
         ],
         compiler_params=pltpu.CompilerParams(vmem_limit_bytes=63_000_000),
         name="tile_rows",

time: 63.3 us -> 53.6 us (0.85)
  Pallas kernels: 61.5 us -> 51.8 us
    pallas_call x1, Pallas kernels: 33.3 us -> 23.6 us  [tile_rows(): pl.pallas_call(functools.partial(tile_kernel, user_dev, sub_dev), out_sha...]
where the time goes in v2:
time: 53.6 us; the launch traced here: 53.2 us
  Pallas kernels  51.8 us (97%)
  local copies, waits for them, and re-layouts  1.38 us (3%)
    pallas_call x1, Pallas kernels, tile_rows(): pl.pallas_call(functools.partial(tile_kernel, user_dev, sub_dev), out_sha...  23.6 us
    pallas_call x1, Pallas kernels, gather_tables(): pl.pallas_call(functools.partial(gather_kernel, n_grp, n_dev), out_shape=...  18.1 us
    pallas_call x1, Pallas kernels, exchange(): pl.pallas_call(functools.partial(exchange_kernel, n_grp, n_dev, cols), ou...  10.1 us
    unnamed x1, local copies, waits for them, and re-layouts  1.38 us

profile of v2, /device:TPU:0, one launch (start us, length us, event | category | flops | bytes accessed | tf_op | source)
XLA Modules:
  0.0 53.2 jit_solution(5393217602295598075)
XLA Ops:
  0.0 18.1 %gather_tables.1.tab_ref = bf16[4,8,160,128]{3,2,1,0:T(8,128)(2,1)} custom-call(bf16[64,1024]{1,0:T(8,128)(2,1)} %uf_ref.1, bf16[64,256]{1,0:T(8,128)(2,1)} %sf_ref.1), custom_call_target="tpu_custom_call" | custom-call | tf_op jit(solution)/shard_map/gather_tables/pallas_call | solution.py:82
  18.1 23.6 %tile_rows.1.rows_ref = f32[128,128]{1,0:T(8,128)} custom-call(bf16[4,8,160,128]{3,2,1,0:T(8,128)(2,1)} %gather_tables.1.tab_ref, f32[128,128]{1,0:T(8,128)} %val_ref.1, s32[128,128]{1,0:T(8,128)} %user_hbm.1, s32[128,128]{1,0:T(8,128)} %sub_hbm.1, s32[128]{0:T(128)} %word_hbm.1, s32[2048]{0:T(1024)} %owner_hbm.1), custom_call_target="tpu_custom_call" | custom-call | tf_op jit(solution)/shard_map/tile_rows/pallas_call | solution.py:182
  41.7 10.1 %exchange.1 = f32[64,64]{1,0:T(8,128)} custom-call(f32[128,128]{1,0:T(8,128)} %tile_rows.1.rows_ref), custom_call_target="tpu_custom_call" | custom-call | tf_op jit(solution)/shard_map/exchange/pallas_call | solution.py:271
  51.9 1.4 %copy.9 = f32[64,64]{1,0:T(8,128)} copy(f32[64,64]{1,0:T(8,128)} %exchange.1) | data formatting | bytes 32768

commit v3 on v2

v3 whole, which is shorter than its diff:
```python
import functools
import jax
import jax.numpy as jnp
from jax import lax
from jax.experimental import pallas as pl
from jax.experimental.pallas import tpu as pltpu

CAP = 2
LANES = 128
VMEM = pltpu.VMEM
HIGH = lax.Precision.HIGHEST
MESH = pl.DeviceIdType.MESH


def packed(x):
    half = x.shape[1] // 2
    x = x.astype(jnp.float32)
    return jnp.concatenate([x[:, :half], x[:, half:]], axis=0).T.astype(jnp.bfloat16)


def where_is(n_dev, p):
    return (p // n_dev, lax.rem(p, n_dev))


def gather_tables(n_grp, n_dev, uf_ref, sf_ref, tab, arrived, barrier_wait,
                  send_a, recv_a, send_b, recv_b, send_c, recv_c):
    grp, dev = lax.axis_index("grp"), lax.axis_index("dev")
    pairs = n_dev // 2
    pos, core = dev // 2, lax.rem(dev, 2)
    sibling = dev + 1 - 2 * core
    rows = tab.shape[2]
    order = sorted(range(1, pairs), key=lambda k: min(k, pairs - k))
    others = [((pos + k) % pairs) for k in order]
    groups = [lax.rem(grp + j, n_grp) for j in range(1, n_grp)]
    block = jnp.concatenate([packed(uf_ref[...]), packed(sf_ref[...])], axis=0)
    for q in range(n_grp):
        tab[q, dev] = block[q * rows:(q + 1) * rows]
    barrier_wait()

    def copy(q, d, send, recv, to):
        return pltpu.make_async_remote_copy(
            src_ref=tab.at[q, d], dst_ref=tab.at[q, d], send_sem=send, recv_sem=recv,
            device_id=to, device_id_type=MESH)

    sent = []

    def start(c):
        c.start()
        sent.append(c)

    def to_sibling(q, p):
        start(copy(q, 2 * p + core, send_c.at[q, p], recv_c.at[q, p], (grp, sibling)))

    for p in others:
        start(copy(grp, dev, send_a.at[p], recv_a.at[pos], (grp, 2 * p + core)))
    for q in range(n_grp):
        to_sibling(q, pos)
    arrived(dev)
    for p in others:
        d = 2 * p + core
        copy(grp, d, send_a.at[p], recv_a.at[p], (grp, d)).wait_recv()
        for g in groups:
            start(copy(grp, d, send_b.at[g, p], recv_b.at[grp, p], (g, dev)))
        to_sibling(grp, p)
    for q in range(n_grp):
        copy(q, sibling, send_c.at[q, pos], recv_c.at[q, pos], (grp, sibling)).wait_recv()
    arrived(sibling)
    for p in others:
        d = 2 * p + core
        for g in groups:
            copy(g, d, send_b.at[g, p], recv_b.at[g, p], (g, dev)).wait_recv()
            to_sibling(g, p)
        arrived(d)
    for p in others:
        d = 2 * p + (1 - core)
        for q in range(n_grp):
            copy(q, d, send_c.at[q, p], recv_c.at[q, p], (grp, sibling)).wait_recv()
        arrived(d)
    return sent


def fill_tables(tab_ref, d, user_dev, sub_dev, utab, stab):
    n_grp, _, rows, lanes = tab_ref.shape
    rank = lanes // 2
    user_half, sub_half = user_dev // 2, sub_dev // 2
    for q in range(n_grp):
        lo, hi = q * rows, (q + 1) * rows
        for table, first, last, size in ((utab, 0, user_half, user_dev),
                                         (stab, user_half, user_half + sub_half, sub_dev)):
            a, b = max(lo, first), min(hi, last)
            if a >= b:
                continue
            x = tab_ref[q, d, a - lo:b - lo, :].astype(jnp.float32)
            base = d * size + (a - first)
            table[pl.ds(pl.multiple_of(base, 8), b - a), :] = x
            table[pl.ds(pl.multiple_of(base + size // 2, 8), b - a), :] = pltpu.roll(x, rank, 1)


STEP = 8


def index_copies(c, half, user_hbm, sub_hbm, users, subs, sems):
    rows = pl.ds(pl.multiple_of(c * STEP, STEP), STEP)
    return [pltpu.make_async_copy(user_hbm.at[rows], users[half], sems.at[half, 0]),
            pltpu.make_async_copy(sub_hbm.at[rows], subs[half], sems.at[half, 1])]


def sum_tiles(user_hbm, sub_hbm, val_ref, words, owners, out_ref, utab, stab, prod, users, subs, sems):
    tiles, lanes = out_ref.shape
    rank = lanes // 2
    width = val_ref.shape[1]
    chunks = tiles // STEP
    lane = lax.broadcasted_iota(jnp.int32, (1, lanes), 1)

    def chunk(c, half):
        for copy in index_copies(c, half, user_hbm, sub_hbm, users, subs, sems):
            copy.wait()
        base = pl.multiple_of(c * STEP, STEP)
        vals = val_ref[pl.ds(base, STEP), :].T
        out = []
        for j in range(STEP):
            for n in range(width):
                u, s = users[half][j, n], subs[half][j, n]
                prod[j % 2, n:n + 1, :] = utab[pl.ds(u, 1), :] * stab[pl.ds(s, 1), :]
            row = jnp.sum(prod[j % 2] * vals[:, j:j + 1], axis=0, keepdims=True)
            owner = owners[words[base + j]].astype(jnp.float32)
            out.append(jnp.where(lane < rank, row, owner))
        out_ref[pl.ds(base, STEP), :] = jnp.concatenate(out, axis=0)

    def two_chunks(i, carry):
        for half in range(2):
            c = 2 * i + half
            chunk(c, half)

            @pl.when(i < chunks // 2 - 1)
            def _():
                for copy in index_copies(c + 2, half, user_hbm, sub_hbm, users, subs, sems):
                    copy.start()
        return carry

    lax.fori_loop(0, chunks // 2, two_chunks, 0)


def tdot(a, b):
    return lax.dot_general(a, b, (((0,), (0,)), ((), ())), precision=HIGH,
                           preferred_element_type=jnp.float32)


def exchange(n_grp, n_dev, cols, rows_ref, out_ref, outbox, inbox, send_sem, recv_sem):
    n_all = n_grp * n_dev
    me = lax.axis_index("grp") * n_dev + lax.axis_index("dev")
    peers = [lax.rem(me + k, n_all) for k in range(1, n_all)]
    rows = rows_ref[...]
    tiles, lanes = rows.shape
    rank = lanes // 2
    lane = lax.broadcasted_iota(jnp.int32, (tiles, lanes), 1)
    owner_row = jnp.where(lane < rank, pltpu.roll(rows, rank, 1), rows).astype(jnp.int32)
    owner = owner_row // cols
    local = owner_row - owner * cols
    slots = n_all * CAP
    slot = lax.broadcasted_iota(jnp.int32, (tiles, slots), 1)
    own_col = owner_row[:, :1]
    owner_col = jnp.broadcast_to(owner[:, :1], (tiles, slots))
    going = jnp.where((owner_col != me) & (owner_col == slot // CAP), 1.0, 0.0)
    earlier = jnp.where(lax.broadcasted_iota(jnp.int32, (tiles, tiles), 0)
                        > lax.broadcasted_iota(jnp.int32, (tiles, tiles), 1), 1.0, 0.0)
    before = jnp.dot(earlier.astype(jnp.bfloat16), going.astype(jnp.bfloat16),
                     preferred_element_type=jnp.float32)
    table = jnp.where(before == (slot - slot // CAP * CAP).astype(jnp.float32), going, 0.0)
    tagged = jnp.where(lane < rank, rows, (local + 1).astype(jnp.float32))
    box = tdot(table, tagged)
    for p in range(n_all):
        outbox[p] = box[p * CAP:(p + 1) * CAP]
    inbox[me] = jnp.zeros((CAP, lanes), jnp.float32)
    copies = []
    for p in peers:
        c = pltpu.make_async_remote_copy(
            src_ref=outbox.at[p], dst_ref=inbox.at[me], send_sem=send_sem.at[p],
            recv_sem=recv_sem.at[me], device_id=where_is(n_dev, p), device_id_type=MESH)
        c.start()
        copies.append(c)
    col = lax.broadcasted_iota(jnp.int32, (tiles, lanes), 1)
    mine = jnp.where(owner_row == me * cols + col, 1.0, 0.0)
    own_part = tdot(rows, mine)
    for p in peers:
        pltpu.make_async_remote_copy(
            src_ref=outbox.at[p], dst_ref=inbox.at[p], send_sem=send_sem.at[p],
            recv_sem=recv_sem.at[p], device_id=where_is(n_dev, p), device_id_type=MESH).wait_recv()
    got = jnp.concatenate([inbox[p] for p in range(n_all)], axis=0)
    glane = lax.broadcasted_iota(jnp.int32, (slots, lanes), 1)
    got_row = jnp.where(glane < rank, pltpu.roll(got, rank, 1), got).astype(jnp.int32)
    far_part = tdot(got, jnp.where(got_row == glane + 1, 1.0, 0.0))
    out_ref[...] = (own_part + far_part)[:rank, :cols]
    for c in copies:
        c.wait_send()


def kernel(n_grp, n_dev, cols, uf_ref, sf_ref, val_ref, user_hbm, sub_hbm, word_hbm, owner_hbm, out_ref,
           tab, utab, stab, prod, users_a, users_b, subs_a, subs_b, words, owners, tile_sums, outbox, inbox,
           sems, word_sems, send_a, recv_a, send_b, recv_b, send_c, recv_c, send_x, recv_x):
    n_all = n_grp * n_dev
    me = lax.axis_index("grp") * n_dev + lax.axis_index("dev")
    barrier = pltpu.get_barrier_semaphore()
    for k in range(1, n_all):
        pl.semaphore_signal(barrier, inc=1, device_id=where_is(n_dev, lax.rem(me + k, n_all)),
                            device_id_type=MESH)
    users, subs = (users_a, users_b), (subs_a, subs_b)
    copies = [pltpu.make_async_copy(word_hbm, words, word_sems.at[0]),
              pltpu.make_async_copy(owner_hbm, owners, word_sems.at[1])]
    for half in range(2):
        for c in index_copies(half, half, user_hbm, sub_hbm, users, subs, sems):
            c.start()
    for c in copies:
        c.start()

    def arrived(d):
        fill_tables(tab, d, uf_ref.shape[1], sf_ref.shape[1], utab, stab)

    sent = gather_tables(n_grp, n_dev, uf_ref, sf_ref, tab, arrived,
                         lambda: pl.semaphore_wait(barrier, n_all - 1),
                         send_a, recv_a, send_b, recv_b, send_c, recv_c)
    for c in copies:
        c.wait()
    sum_tiles(user_hbm, sub_hbm, val_ref, words, owners, tile_sums, utab, stab, prod, users, subs, sems)
    exchange(n_grp, n_dev, cols, tile_sums, out_ref, outbox, inbox, send_x, recv_x)
    for c in sent:
        c.wait_send()


def mttkrp(n_grp, n_dev, nz_user, nz_sub, nz_value, tile_word, word_owner, uf, sf):
    n_all, pairs = n_grp * n_dev, n_dev // 2
    tiles, width = nz_user.shape
    rank, user_dev = uf.shape
    sub_dev = sf.shape[1]
    cols = word_owner.shape[0] // n_all
    rows = (user_dev + sub_dev) // 2 // n_grp
    any_spec = pl.BlockSpec(memory_space=pl.ANY)
    vmem = pl.BlockSpec(memory_space=VMEM)
    dma = pltpu.SemaphoreType.DMA
    return pl.pallas_call(
        functools.partial(kernel, n_grp, n_dev, cols),
        out_shape=jax.ShapeDtypeStruct((rank, cols), jnp.float32),
        in_specs=[vmem, vmem, vmem, any_spec, any_spec, any_spec, any_spec],
        out_specs=vmem,
        scratch_shapes=[
            VMEM((n_grp, n_dev, rows, LANES), jnp.bfloat16),
            VMEM((user_dev * n_dev, LANES), jnp.float32),
            VMEM((sub_dev * n_dev, LANES), jnp.float32),
            VMEM((2, width, LANES), jnp.float32),
            pltpu.SMEM((STEP, width), jnp.int32),
            pltpu.SMEM((STEP, width), jnp.int32),
            pltpu.SMEM((STEP, width), jnp.int32),
            pltpu.SMEM((STEP, width), jnp.int32),
            pltpu.SMEM(tile_word.shape, jnp.int32),
            pltpu.SMEM(word_owner.shape, jnp.int32),
            VMEM((tiles, LANES), jnp.float32),
            VMEM((n_all, CAP, LANES), jnp.float32),
            VMEM((n_all, CAP, LANES), jnp.float32),
            dma((2, 2)), dma((2,)), dma((pairs,)), dma((pairs,)), dma((n_grp, pairs)), dma((n_grp, pairs)),
            dma((n_grp, pairs)), dma((n_grp, pairs)), dma((n_all,)), dma((n_all,)),
        ],
        compiler_params=pltpu.CompilerParams(collective_id=0, has_side_effects=True,
                                             vmem_limit_bytes=63_000_000),
        name="mttkrp",
    )(uf, sf, nz_value, nz_user, nz_sub, tile_word, word_owner)


def solution(mesh):
    n_grp, n_dev = mesh.shape["grp"], mesh.shape["dev"]

    def shards(nz_user, nz_sub, nz_value, tile_word, word_owner, user_factor, sub_factor):
        return mttkrp(n_grp, n_dev, nz_user, nz_sub, nz_value, tile_word, word_owner,
                      user_factor, sub_factor)

    return jax.shard_map(
        shards,
        mesh=mesh,
        in_specs=(
            jax.sharding.PartitionSpec(("grp", "dev"), None),
            jax.sharding.PartitionSpec(("grp", "dev"), None),
            jax.sharding.PartitionSpec(("grp", "dev"), None),
            jax.sharding.PartitionSpec(("grp", "dev")),
            jax.sharding.PartitionSpec(),
            jax.sharding.PartitionSpec(None, "dev"),
            jax.sharding.PartitionSpec(None, "dev"),
        ),
        out_specs=jax.sharding.PartitionSpec(None, ("grp", "dev")),
        check_vma=False,
    )
```

time: 53.6 us -> 49.6 us (0.925)
  Pallas kernels: 51.8 us -> 48.1 us
    pallas_call x3 -> x1, Pallas kernels: 51.8 us -> 48.1 us  [mttkrp(): pl.pallas_call(functools.partial(kernel, n_grp, n_dev, cols), out_shape=j...]
where the time goes in v3:
time: 49.6 us; the launch traced here: 49.4 us
  Pallas kernels  48.1 us (97%)
  local copies, waits for them, and re-layouts  1.38 us (3%)
    pallas_call x1, Pallas kernels, mttkrp(): pl.pallas_call(functools.partial(kernel, n_grp, n_dev, cols), out_shape=j...  48.1 us
    unnamed x1, local copies, waits for them, and re-layouts  1.38 us

profile of v3, /device:TPU:0, one launch (start us, length us, event | category | flops | bytes accessed | tf_op | source)
XLA Modules:
  0.0 49.4 jit_solution(4926788622758204739)
XLA Ops:
  0.0 48.1 %mttkrp.1 = f32[64,64]{1,0:T(8,128)} custom-call(bf16[64,1024]{1,0:T(8,128)(2,1)} %uf_ref.1, bf16[64,256]{1,0:T(8,128)(2,1)} %sf_ref.1, f32[128,128]{1,0:T(8,128)} %val_ref.1, s32[128,128]{1,0:T(8,128)} %user_hbm.1, s32[128,128]{1,0:T(8,128)} %sub_hbm.1, s32[128]{0:T(128)} %word_hbm.1, s32[2048]{0:T(1024)} %owner_hbm.1), custom_call_target="tpu_custom_call" | custom-call | tf_op jit(solution)/shard_map/mttkrp/pallas_call | solution.py:240
  48.1 1.4 %copy.9 = f32[64,64]{1,0:T(8,128)} copy(f32[64,64]{1,0:T(8,128)} %mttkrp.1) | data formatting | bytes 32768

commit v4 on v3

--- a/solution.py
+++ b/solution.py
@@ -79,50 +79,79 @@
     return sent
 
 
-def fill_tables(tab_ref, d, user_dev, sub_dev, utab, stab):
-    n_grp, _, rows, lanes = tab_ref.shape
-    rank = lanes // 2
-    user_half, sub_half = user_dev // 2, sub_dev // 2
+def pieces(n_grp, rows, first, last):
     for q in range(n_grp):
-        lo, hi = q * rows, (q + 1) * rows
-        for table, first, last, size in ((utab, 0, user_half, user_dev),
-                                         (stab, user_half, user_half + sub_half, sub_dev)):
-            a, b = max(lo, first), min(hi, last)
-            if a >= b:
-                continue
-            x = tab_ref[q, d, a - lo:b - lo, :].astype(jnp.float32)
-            base = d * size + (a - first)
-            table[pl.ds(pl.multiple_of(base, 8), b - a), :] = x
-            table[pl.ds(pl.multiple_of(base + size // 2, 8), b - a), :] = pltpu.roll(x, rank, 1)
+        a, b = max(q * rows, first), min((q + 1) * rows, last)
+        if a < b:
+            yield q, a, b
+
+
+def fill_users(tab, d, user_dev, utab):
+    n_grp, _, rows, lanes = tab.shape
+    half = user_dev // 2
+    for q, a, b in pieces(n_grp, rows, 0, half):
+        x = tab[q, d, a - q * rows:b - q * rows, :].astype(jnp.float32)
+        y = pltpu.roll(x, lanes // 2, 1)
+        left = lax.broadcasted_iota(jnp.int32, x.shape, 1) < lanes // 2
+        base = d * user_dev + a
+        utab[pl.ds(pl.multiple_of(base, 8), b - a), :] = jnp.where(left, x, y)
+        utab[pl.ds(pl.multiple_of(base + half, 8), b - a), :] = jnp.where(left, y, x)
+
+
+def fill_subs(tab, user_dev, sub_dev, stab):
+    n_grp, n_dev, rows, lanes = tab.shape
+    start, half = user_dev // 2, sub_dev // 2
+    for q, a, b in pieces(n_grp, rows, start, start + half):
+        for p in range(n_dev // 2):
+            even, odd = [tab[q, 2 * p + i, a - q * rows:b - q * rows, :].astype(jnp.float32) for i in range(2)]
+            left = lax.broadcasted_iota(jnp.int32, even.shape, 1) < lanes // 2
+            at = pl.ds(p * lanes, lanes)
+            low = jnp.where(left, even, pltpu.roll(odd, lanes // 2, 1))
+            high = jnp.where(left, pltpu.roll(even, lanes // 2, 1), odd)
+            stab[a - start:b - start, at] = low.astype(jnp.bfloat16)
+            stab[half + a - start:half + b - start, at] = high.astype(jnp.bfloat16)
 
 
 STEP = 8
 
 
-def index_copies(c, half, user_hbm, sub_hbm, users, subs, sems):
+def index_copies(c, half, user_hbm, users, sems):
     rows = pl.ds(pl.multiple_of(c * STEP, STEP), STEP)
-    return [pltpu.make_async_copy(user_hbm.at[rows], users[half], sems.at[half, 0]),
-            pltpu.make_async_copy(sub_hbm.at[rows], subs[half], sems.at[half, 1])]
-
-
-def sum_tiles(user_hbm, sub_hbm, val_ref, words, owners, out_ref, utab, stab, prod, users, subs, sems):
+    return [pltpu.make_async_copy(user_hbm.at[rows], users[half], sems.at[half])]
+
+
+def sum_tiles(user_hbm, sub_ref, val_ref, words, owners, out_ref, utab, stab, picked, users, sems):
     tiles, lanes = out_ref.shape
     rank = lanes // 2
     width = val_ref.shape[1]
     chunks = tiles // STEP
+    depth, wide = stab.shape
     lane = lax.broadcasted_iota(jnp.int32, (1, lanes), 1)
+    lanes_of = lax.broadcasted_iota(jnp.int32, (width, lanes), 1)
+    side = jnp.where(lanes_of < rank, 0, 1)
+    keys = lax.broadcasted_iota(jnp.int32, (width, depth), 1)
 
     def chunk(c, half):
-        for copy in index_copies(c, half, user_hbm, sub_hbm, users, subs, sems):
+        for copy in index_copies(c, half, user_hbm, users, sems):
             copy.wait()
         base = pl.multiple_of(c * STEP, STEP)
         vals = val_ref[pl.ds(base, STEP), :].T
+        subs = sub_ref[pl.ds(base, STEP), :]
+        group = subs // depth
+        key = (subs - group * depth).astype(jnp.float32).T.astype(jnp.int32)
+        group = group.astype(jnp.float32).T.astype(jnp.int32)
         out = []
         for j in range(STEP):
             for n in range(width):
-                u, s = users[half][j, n], subs[half][j, n]
-                prod[j % 2, n:n + 1, :] = utab[pl.ds(u, 1), :] * stab[pl.ds(s, 1), :]
-            row = jnp.sum(prod[j % 2] * vals[:, j:j + 1], axis=0, keepdims=True)
+                picked[j % 2, n:n + 1, :] = utab[pl.ds(users[half][j, n], 1), :]
+            onehot = jnp.where(key[:, j:j + 1] == keys, 1.0, 0.0).astype(jnp.bfloat16)
+            found = jnp.dot(onehot, stab[...], preferred_element_type=jnp.float32)
+            pick = jnp.broadcast_to(group[:, j:j + 1], (width, lanes)) - side
+            sub_rows = jnp.where(pick == 0, found[:, :lanes], 0.0)
+            for p in range(1, wide // lanes):
+                sub_rows = jnp.where(pick == 2 * p, found[:, p * lanes:(p + 1) * lanes], sub_rows)
+            row = jnp.sum(picked[j % 2] * sub_rows * vals[:, j:j + 1], axis=0, keepdims=True)
+            row = row + pltpu.roll(row, rank, 1)
             owner = owners[words[base + j]].astype(jnp.float32)
             out.append(jnp.where(lane < rank, row, owner))
         out_ref[pl.ds(base, STEP), :] = jnp.concatenate(out, axis=0)
@@ -134,7 +163,7 @@
 
             @pl.when(i < chunks // 2 - 1)
             def _():
-                for copy in index_copies(c + 2, half, user_hbm, sub_hbm, users, subs, sems):
+                for copy in index_copies(c + 2, half, user_hbm, users, sems):
                     copy.start()
         return carry
 
@@ -195,8 +224,8 @@
         c.wait_send()
 
 
-def kernel(n_grp, n_dev, cols, uf_ref, sf_ref, val_ref, user_hbm, sub_hbm, word_hbm, owner_hbm, out_ref,
-           tab, utab, stab, prod, users_a, users_b, subs_a, subs_b, words, owners, tile_sums, outbox, inbox,
+def kernel(n_grp, n_dev, cols, uf_ref, sf_ref, val_ref, sub_ref, user_hbm, word_hbm, owner_hbm, out_ref,
+           tab, utab, stab, prod, users_a, users_b, words, owners, tile_sums, outbox, inbox,
            sems, word_sems, send_a, recv_a, send_b, recv_b, send_c, recv_c, send_x, recv_x):
     n_all = n_grp * n_dev
     me = lax.axis_index("grp") * n_dev + lax.axis_index("dev")
@@ -204,24 +233,25 @@
     for k in range(1, n_all):
         pl.semaphore_signal(barrier, inc=1, device_id=where_is(n_dev, lax.rem(me + k, n_all)),
                             device_id_type=MESH)
-    users, subs = (users_a, users_b), (subs_a, subs_b)
+    users = (users_a, users_b)
     copies = [pltpu.make_async_copy(word_hbm, words, word_sems.at[0]),
               pltpu.make_async_copy(owner_hbm, owners, word_sems.at[1])]
     for half in range(2):
-        for c in index_copies(half, half, user_hbm, sub_hbm, users, subs, sems):
+        for c in index_copies(half, half, user_hbm, users, sems):
             c.start()
     for c in copies:
         c.start()
 
     def arrived(d):
-        fill_tables(tab, d, uf_ref.shape[1], sf_ref.shape[1], utab, stab)
+        fill_users(tab, d, uf_ref.shape[1], utab)
 
     sent = gather_tables(n_grp, n_dev, uf_ref, sf_ref, tab, arrived,
                          lambda: pl.semaphore_wait(barrier, n_all - 1),
                          send_a, recv_a, send_b, recv_b, send_c, recv_c)
     for c in copies:
         c.wait()
-    sum_tiles(user_hbm, sub_hbm, val_ref, words, owners, tile_sums, utab, stab, prod, users, subs, sems)
+    fill_subs(tab, uf_ref.shape[1], sf_ref.shape[1], stab)
+    sum_tiles(user_hbm, sub_ref, val_ref, words, owners, tile_sums, utab, stab, prod, users, sems)
     exchange(n_grp, n_dev, cols, tile_sums, out_ref, outbox, inbox, send_x, recv_x)
     for c in sent:
         c.wait_send()
@@ -240,15 +270,13 @@
     return pl.pallas_call(
         functools.partial(kernel, n_grp, n_dev, cols),
         out_shape=jax.ShapeDtypeStruct((rank, cols), jnp.float32),
-        in_specs=[vmem, vmem, vmem, any_spec, any_spec, any_spec, any_spec],
+        in_specs=[vmem, vmem, vmem, vmem, any_spec, any_spec, any_spec],
         out_specs=vmem,
         scratch_shapes=[
             VMEM((n_grp, n_dev, rows, LANES), jnp.bfloat16),
             VMEM((user_dev * n_dev, LANES), jnp.float32),
-            VMEM((sub_dev * n_dev, LANES), jnp.float32),
+            VMEM((sub_dev, n_dev * rank), jnp.bfloat16),
             VMEM((2, width, LANES), jnp.float32),
-            pltpu.SMEM((STEP, width), jnp.int32),
-            pltpu.SMEM((STEP, width), jnp.int32),
             pltpu.SMEM((STEP, width), jnp.int32),
             pltpu.SMEM((STEP, width), jnp.int32),
             pltpu.SMEM(tile_word.shape, jnp.int32),
@@ -256,13 +284,13 @@
             VMEM((tiles, LANES), jnp.float32),
             VMEM((n_all, CAP, LANES), jnp.float32),
             VMEM((n_all, CAP, LANES), jnp.float32),
-            dma((2, 2)), dma((2,)), dma((pairs,)), dma((pairs,)), dma((n_grp, pairs)), dma((n_grp, pairs)),
+            dma((2,)), dma((2,)), dma((pairs,)), dma((pairs,)), dma((n_grp, pairs)), dma((n_grp, pairs)),
             dma((n_grp, pairs)), dma((n_grp, pairs)), dma((n_all,)), dma((n_all,)),
         ],
         compiler_params=pltpu.CompilerParams(collective_id=0, has_side_effects=True,
                                              vmem_limit_bytes=63_000_000),
         name="mttkrp",
-    )(uf, sf, nz_value, nz_user, nz_sub, tile_word, word_owner)
+    )(uf, sf, nz_value, nz_sub, nz_user, tile_word, word_owner)
 
 
 def solution(mesh):

time: 49.6 us -> 50.6 us (1.020)
  Pallas kernels: 48.1 us -> 49 us
    pallas_call x1, Pallas kernels: 48.1 us -> 49 us  [mttkrp(): pl.pallas_call(functools.partial(kernel, n_grp, n_dev, cols), out_shape=j...]
where the time goes in v4:
time: 50.6 us; the launch traced here: 50.4 us
  Pallas kernels  49 us (97%)
  local copies, waits for them, and re-layouts  1.38 us (3%)
    pallas_call x1, Pallas kernels, mttkrp(): pl.pallas_call(functools.partial(kernel, n_grp, n_dev, cols), out_shape=j...  49 us
    unnamed x1, local copies, waits for them, and re-layouts  1.38 us

profile of v4, /device:TPU:0, one launch (start us, length us, event | category | flops | bytes accessed | tf_op | source)
XLA Modules:
  0.0 50.4 jit_solution(17074865312111434049)
XLA Ops:
  0.0 49.0 %mttkrp.1 = f32[64,64]{1,0:T(8,128)} custom-call(bf16[64,1024]{1,0:T(8,128)(2,1)} %uf_ref.1, bf16[64,256]{1,0:T(8,128)(2,1)} %sf_ref.1, f32[128,128]{1,0:T(8,128)} %val_ref.1, s32[128,128]{1,0:T(8,128)} %sub_ref.1, s32[128,128]{1,0:T(8,128)} %user_hbm.1, s32[128]{0:T(128)} %word_hbm.1, s32[2048]{0:T(1024)} %owner_hbm.1), custom_call_target="tpu_custom_call" | custom-call | tf_op jit(solution)/shard_map/mttkrp/pallas_call | solution.py:270
  49.0 1.4 %copy.9 = f32[64,64]{1,0:T(8,128)} copy(f32[64,64]{1,0:T(8,128)} %mttkrp.1) | data formatting | bytes 32768
